TPU v7x, 32 devices: a whole 2x2x4 slice. The times are simulated.
32 devices in a mesh: seq: 8 (over z, core), tp: 2 (over y), dp: 2 (over x).
Axes of the slice: x: 2, y: 2, z: 4, core: 2. Of those that a mesh axis runs over, the one named last changes fastest.
Arguments:
- query_latent: bfloat16 [2, 2048, 1536], P('dp', 'seq', 'tp'), may hold values from -6 to 6
- key_latent: bfloat16 [2, 2048, 512], P('dp', 'seq', 'tp'), may hold values from -6 to 6
- rope_key: bfloat16 [2, 2048, 64], P('dp', 'seq'), may hold values from -6 to 6
- w_uq: bfloat16 [1536, 12288], P('seq', 'tp')
- w_uk: bfloat16 [512, 8192], P('seq', 'tp'), may hold values from -0.25 to 0.25
- w_uv: bfloat16 [512, 8192], P('seq', 'tp'), may hold values from -0.25 to 0.25
- block_order: int32 [2, 16], P('dp'), may hold values from 0 to 15, each once within a row
- segment_ids: int32 [2, 2048], P('dp'), may hold values from 0 to 3, never falling along the last dimension, each value on 1 to 1024 neighbouring positions
Outputs:
- context: bfloat16 [2, 2048, 8192], P('dp', 'seq', 'tp')
- clipped_uq: bfloat16 [1536, 12288], P('seq', 'tp')
- clipped_uk: bfloat16 [512, 8192], P('seq', 'tp')
Inputs may be any that keep to these rules, and one draw needn't show every extreme that they name: `block_order`: each row is a permutation of the 16 position blocks. `segment_ids`: never falling along positions; each document has at most 1024 positions.
All inputs are finite; a program needn't handle non-finite values.
Results may differ from a plain program's by a relative error of at most 0.012.
The roundings to bfloat16 on the way count: a program that leaves them out, or rounds other values in their place, can miss the bound.
Values may be sent and summed in bfloat16 or wider, within the bound.
A program may use at most 128 MiB of HBM per device.

v0:
```python
import math

import jax
import jax.numpy as jnp
from jax import lax
from jax.sharding import PartitionSpec as P

NOPE = 128
ROPE = 64
VD = 128
CLIP = 8


rope_base = 50000.0
masked_value = -1e30


def turning(positions, width):
    steps = jnp.arange(width // 2, dtype=jnp.float32) * (2.0 / width)
    freqs = jnp.exp(-math.log(rope_base) * steps)
    angle = positions.astype(jnp.float32)[:, None] * freqs[None, :]
    return (jnp.cos(angle), jnp.sin(angle))


def rotate(values, cosine, sine):
    half = values.shape[-1] // 2
    first = values[..., :half]
    second = values[..., half:]
    return jnp.concatenate(
        [first * cosine - second * sine, second * cosine + first * sine], axis=-1
    )


def positions_of(index, order, half_block):
    which = index // half_block
    onehot = which[:, None] == jnp.arange(order.shape[0], dtype=jnp.int32)[None, :]
    base = jnp.sum(jnp.where(onehot, order[None, :], 0), axis=1)
    return base * half_block + index % half_block


def on_device(query_latent, key_latent, rope_key, w_uq, w_uk, w_uv, block_order, segment_ids):
    query_local, key_local = (
        lax.all_gather(query_latent[0], "tp", axis=1, tiled=True),
        lax.all_gather(key_latent[0], "tp", axis=1, tiled=True),
    )
    rows_uq, rows_uk, rows_uv = (
        lax.all_gather(w_uq, "seq", axis=0, tiled=True),
        lax.all_gather(w_uk, "seq", axis=0, tiled=True),
        lax.all_gather(w_uv, "seq", axis=0, tiled=True),
    )
    tok_rows = query_local.shape[0]
    half_block = tok_rows // 2
    order = block_order[0]
    labels_all = segment_ids[0]
    heads = w_uq.shape[1] // (NOPE + ROPE)
    scale = 1.0 / math.sqrt(NOPE + ROPE)
    own_index = lax.axis_index("seq") * tok_rows + jnp.arange(tok_rows, dtype=jnp.int32)
    query_pos = positions_of(own_index, order, half_block)
    query_labels = jnp.take(labels_all, query_pos)
    cosine, sine = turning(query_pos, ROPE)
    query_full = jnp.dot(query_local, rows_uq, preferred_element_type=jnp.float32).reshape(
        tok_rows, heads, NOPE + ROPE
    )
    query_nope = jnp.transpose(query_full[:, :, :NOPE].astype(jnp.bfloat16), (1, 0, 2))
    query_rope = jnp.transpose(
        rotate(query_full[:, :, NOPE:], cosine[:, None, :], sine[:, None, :]).astype(jnp.bfloat16),
        (1, 0, 2),
    )
    key_rope = rotate(rope_key[0].astype(jnp.float32), cosine, sine).astype(jnp.bfloat16)

    def slice_latent(pieces, first, width):
        latent_block = lax.dynamic_slice_in_dim(pieces[0], first, width, 0)
        rope_block = lax.dynamic_slice_in_dim(pieces[1], first, width, 0)
        nope_block = jnp.dot(latent_block, rows_uk, preferred_element_type=jnp.float32).astype(
            jnp.bfloat16
        )
        value_block = jnp.dot(latent_block, rows_uv, preferred_element_type=jnp.float32).astype(
            jnp.bfloat16
        )
        return (nope_block, value_block, rope_block)

    initial = (
        jnp.full((heads, tok_rows), masked_value, jnp.float32),
        jnp.zeros((heads, tok_rows), jnp.float32),
        jnp.zeros((heads, tok_rows, VD), jnp.float32),
    )
    pieces = (
        lax.all_gather(key_local, "seq", axis=0, tiled=True),
        lax.all_gather(key_rope, "seq", axis=0, tiled=True),
    )
    count = pieces[-1].shape[0]
    width = math.gcd(count, 512)

    def block_step(state, number):
        first = number * width
        nope_block, value_block, rope_block = slice_latent(pieces, first, width)
        nope_block = nope_block.reshape(width, heads, NOPE)
        value_block = value_block.reshape(width, heads, VD)
        key_index = first + jnp.arange(width, dtype=jnp.int32)
        key_pos = positions_of(key_index, order, half_block)
        key_labels = jnp.take(labels_all, key_pos)
        allowed = (key_pos[None, :] <= query_pos[:, None]) & (
            key_labels[None, :] == query_labels[:, None]
        )
        scores = jnp.einsum(
            "hqd,khd->hqk", query_nope, nope_block, preferred_element_type=jnp.float32
        )
        scores = (
            scores
            + jnp.einsum("hqr,kr->hqk", query_rope, rope_block, preferred_element_type=jnp.float32)
        ) * scale
        masked = jnp.where(allowed[None], scores, masked_value)
        run_max, run_total, run_sum = state
        new_max = jnp.maximum(run_max, jnp.max(masked, axis=2))
        weights = jnp.where(allowed[None], jnp.exp(masked - new_max[:, :, None]), 0.0)
        shrink = jnp.exp(run_max - new_max)
        new_total = run_total * shrink + jnp.sum(weights, axis=2)
        mixed = jnp.einsum(
            "hqk,khv->hqv",
            weights.astype(jnp.bfloat16),
            value_block,
            preferred_element_type=jnp.float32,
        )
        new_sum = run_sum * shrink[:, :, None] + mixed
        return ((new_max, new_total, new_sum), None)

    result, unused = lax.scan(block_step, initial, jnp.arange(count // width, dtype=jnp.int32))
    run_max, run_total, run_sum = result
    context = (run_sum / run_total[:, :, None]).astype(jnp.bfloat16)
    context = jnp.transpose(context, (1, 0, 2)).reshape(1, tok_rows, heads * VD)
    head_max = lax.pmax(jnp.max(run_max, axis=1), ("seq", "dp"))
    ratio = CLIP / jnp.maximum(head_max, CLIP)
    root = jnp.sqrt(ratio)
    factors = jnp.concatenate(
        [
            jnp.broadcast_to(root[:, None], (heads, NOPE)),
            jnp.broadcast_to(ratio[:, None], (heads, ROPE)),
        ],
        axis=1,
    ).reshape(heads * (NOPE + ROPE))
    clipped_uq = (w_uq.astype(jnp.float32) * factors[None, :]).astype(jnp.bfloat16)
    clipped_uk = (w_uk.astype(jnp.float32) * jnp.repeat(root, NOPE)[None, :]).astype(jnp.bfloat16)
    return (context, clipped_uq, clipped_uk)


def solution(mesh):
    placed = (
        P("dp", "seq", "tp"),
        P("dp", "seq", "tp"),
        P("dp", "seq", None),
        P("seq", "tp"),
        P("seq", "tp"),
        P("seq", "tp"),
        P("dp", None),
        P("dp", None),
    )
    return jax.shard_map(
        on_device,
        mesh=mesh,
        in_specs=placed,
        out_specs=(P("dp", "seq", "tp"), P("seq", "tp"), P("seq", "tp")),
        check_vma=False,
    )
```

profile of v0, /device:TPU:9, one launch (start us, length us, event | category | flops | bytes accessed | tf_op | source)
XLA Modules:
  0.0 553.9 jit_solution(4917340522343472896)
XLA Ops:
  8.0 7.0 %all-gather = bf16[1,256,512]{2,1,0:T(8,128)(2,1)} all-gather(bf16[1,256,256]{2,1,0:T(8,128)(2,1)} %param.11), channel_id=2, replica_groups=mesh['seq'=8,'tp'=2,'dp'=2] {'tp'}, dimensions={2}, use_global_device_ids=true | all-gather | bytes 393216 | tf_op jit(solution)/shard_map/all_gather | solution.py:44
  19.1 25.0 %all_gather.26 = bf16[2048,64]{0,1:T(8,128)(2,1)} all-gather(bf16[256,64]{0,1:T(8,128)(2,1)S(1)} %pad_maximum_fusion), channel_id=1, replica_groups=mesh['seq'=8,'tp'=2,'dp'=2] {'seq'}, dimensions={0}, use_global_device_ids=true | all-gather | bytes 294912 | tf_op jit(solution)/shard_map/all_gather | solution.py:89
  44.1 11.3 %all-gather.2 = bf16[1,256,1536]{2,1,0:T(8,128)(2,1)S(1)} all-gather(bf16[1,256,768]{2,1,0:T(8,128)(2,1)S(1)} %copy-done.7), channel_id=4, replica_groups=mesh['seq'=8,'tp'=2,'dp'=2] {'tp'}, dimensions={2}, use_global_device_ids=true | all-gather | bytes 1179648 | tf_op jit(solution)/shard_map/all_gather | solution.py:43
  55.4 123.3 %all-gather.10.cloned.1.call-done = bf16[1536,6144]{1,0:T(8,128)(2,1)} async-done(((bf16[192,6144]{1,0:T(8,128)(2,1)}), bf16[1536,6144]{1,0:T(8,128)(2,1)}) %all-gather.10.cloned.1.call-update) | async-done | bytes 18874384 | tf_op jit(solution)/shard_map/all_gather | solution.py:47
  178.7 11.8 %fusion.38 = f32[256,6144]{0,1:T(8,128)S(1)} fusion(bf16[1536,6144]{1,0:T(8,128)(2,1)} %all-gather.10.cloned.1.call-done, bf16[1,256,1536]{2,1,0:T(8,128)(2,1)S(1)} %all-gather.2), kind=kOutput, calls=%fused_computation.68 | convolution fusion | flops 4831838208 | bytes 25952256 | tf_op jit(solution)/shard_map/dot_general | solution.py:61
  199.3 11.0 %all-gather.14.cloned.1.call-done = bf16[1,2048,512]{2,1,0:T(8,128)(2,1)} async-done(((bf16[1,256,512]{2,1,0:T(8,128)(2,1)}), bf16[1,2048,512]{2,1,0:T(8,128)(2,1)}) %all-gather.14.cloned.1.call-update) | async-done | bytes 2097168 | tf_op jit(solution)/shard_map/all_gather | solution.py:88
  210.2 46.7 %all-gather.12.cloned.1.call-done = bf16[512,4096]{1,0:T(8,128)(2,1)} async-done(((bf16[64,4096]{1,0:T(8,128)(2,1)}), bf16[512,4096]{1,0:T(8,128)(2,1)}) %all-gather.12.cloned.1.call-update) | async-done | bytes 4194320 | tf_op jit(solution)/shard_map/all_gather | solution.py:49
  256.9 47.2 %all-gather.8.cloned.1.call-done = bf16[512,4096]{1,0:T(8,128)(2,1)} async-done(((bf16[64,4096]{1,0:T(8,128)(2,1)}), bf16[512,4096]{1,0:T(8,128)(2,1)}) %all-gather.8.cloned.1.call-update) | async-done | bytes 4194320 | tf_op jit(solution)/shard_map/all_gather | solution.py:48
  304.1 205.4 %while.17 = (s32[]{:T(128)}, f32[32,256]{1,0:T(8,128)S(1)}, f32[32,256]{1,0:T(8,128)}, f32[32,256,128]{2,1,0:T(8,128)}, s32[4]{0:T(128)S(1)}, /*index=5*/s32[1,1...) while((s32[]{:T(128)}, f32[32,256]{1,0:T(8,128)S(1)}, ...), condition=%wide.region_5.6_spmd.clone, body=%wide.region_1.5_spmd.clone.sunk | while | flops 7029091840 | bytes 140370992 | solution.py:127
  309.5 6.8 %fusion.84 = bf16[64,32,8,128]{3,2,1,0:T(8,128)(2,1)} fusion(bf16[512,4096]{1,0:T(8,128)(2,1)} %get-tuple-element.478, bf16[2048,512]{1,0:T(8,128)(2,1)} %get-tuple-element.473, s32[]{:T(128)S(6)} %select_n.238), kind=kOutput, calls=%fused_computation.22.clone.1 | convolution fusion | flops 2149580800 | bytes 8912900 | tf_op jit(solution)/shard_map/while/body/eval_jaxpr/dot_general | solution.py:77
  323.7 10.5 %fusion.81 = (f32[32,256]{1,0:T(8,128)S(1)}, f32[32,256,512]{1,2,0:T(8,128)}) fusion(bf16[32,256,64]{1,2,0:T(8,128)(2,1)} %get-tuple-element.477, bf16[2048,64]{0,1:T(8,128)(2,1)} %get-tuple-element.476, s32[]{:T(128)S(6)} %select_n.238, f32[32,512,256]{2,1,0:T(8,128)S(1)} %fusion.80, pred[256,512]{0,1:T(8,128)(4,1)} %compare_and_fusion.2), kind=kOutput, calls=%fused_computation.103.clone.1 | convolution fusion | flops 553639936 | bytes 34832388 | tf_op jit(solution)/shard_map/while/body/eval_jaxpr/hqr,kr->hqk/dot_general | solution.py:110
  334.3 8.7 %fusion.82 = f32[32,256]{1,0:T(8,128)S(1)} fusion(f32[32,256,512]{1,2,0:T(8,128)} %get-tuple-element.423, f32[32,256]{1,0:T(8,128)S(1)} %select_maximum_fusion.2, pred[256,512]{0,1:T(8,128)(4,1)S(1)} %copy-done.1), kind=kLoop, calls=%fused_computation.7.clone.1 | loop fusion | flops 12574720 | bytes 16973824 | tf_op jit(solution)/shard_map/while/body/eval_jaxpr/reduce_sum | solution.py:117
  343.0 11.7 %fusion.85 = f32[32,256,128]{2,1,0:T(8,128)} fusion(f32[32,256,128]{2,1,0:T(8,128)} %get-tuple-element.448, f32[32,256]{1,0:T(8,128)S(1)} %get-tuple-element.425, pred[]{:T(512)S(6)} %compare.37, bf16[64,32,8,128]{3,2,1,0:T(8,128)(2,1)} %fusion.84, f32[32,256,512]{1,2,0:T(8,128)} %get-tuple-element.423, f32[32,256]{1,0:T(8,128)S(1)} %select_maximum_fusion.2, ...), kind=kOutput, calls=%fused_computation.20.clone.1 | convolution fusion | flops 1089470464 | bytes 29556736 | tf_op jit(solution)/shard_map/while/body/eval_jaxpr/hqk,khv->hqv/dot_general | solution.py:118
  374.5 10.5 %fusion.81 = (f32[32,256]{1,0:T(8,128)S(1)}, f32[32,256,512]{1,2,0:T(8,128)}) fusion(bf16[32,256,64]{1,2,0:T(8,128)(2,1)} %get-tuple-element.477, bf16[2048,64]{0,1:T(8,128)(2,1)} %get-tuple-element.476, s32[]{:T(128)S(6)} %select_n.238, f32[32,512,256]{2,1,0:T(8,128)S(1)} %fusion.80, pred[256,512]{0,1:T(8,128)(4,1)} %compare_and_fusion.2), kind=kOutput, calls=%fused_computation.103.clone.1 | convolution fusion | flops 553639936 | bytes 34832388 | tf_op jit(solution)/shard_map/while/body/eval_jaxpr/hqr,kr->hqk/dot_general | solution.py:110
  385.0 8.7 %fusion.82 = f32[32,256]{1,0:T(8,128)S(1)} fusion(f32[32,256,512]{1,2,0:T(8,128)} %get-tuple-element.423, f32[32,256]{1,0:T(8,128)S(1)} %select_maximum_fusion.2, pred[256,512]{0,1:T(8,128)(4,1)S(1)} %copy-done.1), kind=kLoop, calls=%fused_computation.7.clone.1 | loop fusion | flops 12574720 | bytes 16973824 | tf_op jit(solution)/shard_map/while/body/eval_jaxpr/reduce_sum | solution.py:117
  393.8 12.4 %fusion.85 = f32[32,256,128]{2,1,0:T(8,128)} fusion(f32[32,256,128]{2,1,0:T(8,128)} %get-tuple-element.448, f32[32,256]{1,0:T(8,128)S(1)} %get-tuple-element.425, pred[]{:T(512)S(6)} %compare.37, bf16[64,32,8,128]{3,2,1,0:T(8,128)(2,1)} %fusion.84, f32[32,256,512]{1,2,0:T(8,128)} %get-tuple-element.423, f32[32,256]{1,0:T(8,128)S(1)} %select_maximum_fusion.2, ...), kind=kOutput, calls=%fused_computation.20.clone.1 | convolution fusion | flops 1089470464 | bytes 29556736 | tf_op jit(solution)/shard_map/while/body/eval_jaxpr/hqk,khv->hqv/dot_general | solution.py:118
  426.0 10.5 %fusion.81 = (f32[32,256]{1,0:T(8,128)S(1)}, f32[32,256,512]{1,2,0:T(8,128)}) fusion(bf16[32,256,64]{1,2,0:T(8,128)(2,1)} %get-tuple-element.477, bf16[2048,64]{0,1:T(8,128)(2,1)} %get-tuple-element.476, s32[]{:T(128)S(6)} %select_n.238, f32[32,512,256]{2,1,0:T(8,128)S(1)} %fusion.80, pred[256,512]{0,1:T(8,128)(4,1)} %compare_and_fusion.2), kind=kOutput, calls=%fused_computation.103.clone.1 | convolution fusion | flops 553639936 | bytes 34832388 | tf_op jit(solution)/shard_map/while/body/eval_jaxpr/hqr,kr->hqk/dot_general | solution.py:110
  436.5 8.7 %fusion.82 = f32[32,256]{1,0:T(8,128)S(1)} fusion(f32[32,256,512]{1,2,0:T(8,128)} %get-tuple-element.423, f32[32,256]{1,0:T(8,128)S(1)} %select_maximum_fusion.2, pred[256,512]{0,1:T(8,128)(4,1)S(1)} %copy-done.1), kind=kLoop, calls=%fused_computation.7.clone.1 | loop fusion | flops 12574720 | bytes 16973824 | tf_op jit(solution)/shard_map/while/body/eval_jaxpr/reduce_sum | solution.py:117
  445.3 12.4 %fusion.85 = f32[32,256,128]{2,1,0:T(8,128)} fusion(f32[32,256,128]{2,1,0:T(8,128)} %get-tuple-element.448, f32[32,256]{1,0:T(8,128)S(1)} %get-tuple-element.425, pred[]{:T(512)S(6)} %compare.37, bf16[64,32,8,128]{3,2,1,0:T(8,128)(2,1)} %fusion.84, f32[32,256,512]{1,2,0:T(8,128)} %get-tuple-element.423, f32[32,256]{1,0:T(8,128)S(1)} %select_maximum_fusion.2, ...), kind=kOutput, calls=%fused_computation.20.clone.1 | convolution fusion | flops 1089470464 | bytes 29556736 | tf_op jit(solution)/shard_map/while/body/eval_jaxpr/hqk,khv->hqv/dot_general | solution.py:118
  463.2 6.8 %fusion.84 = bf16[64,32,8,128]{3,2,1,0:T(8,128)(2,1)} fusion(bf16[512,4096]{1,0:T(8,128)(2,1)} %get-tuple-element.478, bf16[2048,512]{1,0:T(8,128)(2,1)} %get-tuple-element.473, s32[]{:T(128)S(6)} %select_n.238), kind=kOutput, calls=%fused_computation.22.clone.1 | convolution fusion | flops 2149580800 | bytes 8912900 | tf_op jit(solution)/shard_map/while/body/eval_jaxpr/dot_general | solution.py:77
  477.4 10.5 %fusion.81 = (f32[32,256]{1,0:T(8,128)S(1)}, f32[32,256,512]{1,2,0:T(8,128)}) fusion(bf16[32,256,64]{1,2,0:T(8,128)(2,1)} %get-tuple-element.477, bf16[2048,64]{0,1:T(8,128)(2,1)} %get-tuple-element.476, s32[]{:T(128)S(6)} %select_n.238, f32[32,512,256]{2,1,0:T(8,128)S(1)} %fusion.80, pred[256,512]{0,1:T(8,128)(4,1)} %compare_and_fusion.2), kind=kOutput, calls=%fused_computation.103.clone.1 | convolution fusion | flops 553639936 | bytes 34832388 | tf_op jit(solution)/shard_map/while/body/eval_jaxpr/hqr,kr->hqk/dot_general | solution.py:110
  488.0 8.7 %fusion.82 = f32[32,256]{1,0:T(8,128)S(1)} fusion(f32[32,256,512]{1,2,0:T(8,128)} %get-tuple-element.423, f32[32,256]{1,0:T(8,128)S(1)} %select_maximum_fusion.2, pred[256,512]{0,1:T(8,128)(4,1)S(1)} %copy-done.1), kind=kLoop, calls=%fused_computation.7.clone.1 | loop fusion | flops 12574720 | bytes 16973824 | tf_op jit(solution)/shard_map/while/body/eval_jaxpr/reduce_sum | solution.py:117
  496.8 12.4 %fusion.85 = f32[32,256,128]{2,1,0:T(8,128)} fusion(f32[32,256,128]{2,1,0:T(8,128)} %get-tuple-element.448, f32[32,256]{1,0:T(8,128)S(1)} %get-tuple-element.425, pred[]{:T(512)S(6)} %compare.37, bf16[64,32,8,128]{3,2,1,0:T(8,128)(2,1)} %fusion.84, f32[32,256,512]{1,2,0:T(8,128)} %get-tuple-element.423, f32[32,256]{1,0:T(8,128)S(1)} %select_maximum_fusion.2, ...), kind=kOutput, calls=%fused_computation.20.clone.1 | convolution fusion | flops 1089470464 | bytes 29556736 | tf_op jit(solution)/shard_map/while/body/eval_jaxpr/hqk,khv->hqv/dot_general | solution.py:118
  519.3 25.0 %pmax.7 = f32[32]{0:T(128)S(1)} all-reduce(f32[32]{0:T(128)S(1)} %reduce_max.21), channel_id=1, replica_groups=mesh['seq'=8,'tp'=2,'dp'=2] {'seq','dp'}, use_global_device_ids=true, to_apply=%region_7.8 | all-reduce | flops 32 | bytes 256 | tf_op jit(solution)/shard_map/pmax | solution.py:131
  (199 shorter events, 88.7 us)
Async XLA Ops:
  7.2 36.9 %copy-start.7 = (bf16[1,256,768]{2,1,0:T(8,128)(2,1)S(1)}, bf16[1,256,768]{2,1,0:T(8,128)(2,1)}, u32[]{:S(2)}) copy-start(bf16[1,256,768]{2,1,0:T(8,128)(2,1)} %param.10) | copy-start | bytes 1179652
  7.2 171.5 %all-gather.10.cloned.1.call-start = ((), (), s32[]{:S(2)}) async-start(), calls=%async_computation.1 | async-start | bytes 21233664 | tf_op jit(solution)/shard_map/all_gather | solution.py:47
  7.9 202.3 %all-gather.14.cloned.1.call-start = ((), (), s32[]{:S(2)}) async-start(), calls=%async_computation.3 | async-start | bytes 2359296 | tf_op jit(solution)/shard_map/all_gather | solution.py:88
  15.0 241.9 %all-gather.12.cloned.1.call-start = ((), (), s32[]{:S(2)}) async-start(), calls=%async_computation.2 | async-start | bytes 4718592 | tf_op jit(solution)/shard_map/all_gather | solution.py:49
  15.7 288.4 %all-gather.8.cloned.1.call-start = ((), (), s32[]{:S(2)}) async-start(), calls=%async_computation | async-start | bytes 4718592 | tf_op jit(solution)/shard_map/all_gather | solution.py:48
  193.4 110.7 %copy-start.13 = (s32[1,16]{1,0:T(1,128)S(1)}, s32[1,16]{1,0:T(1,128)}, u32[]{:S(2)}) copy-start(s32[1,16]{1,0:T(1,128)} %param.16) | copy-start | bytes 196
  343.0 11.8 %copy-start.6 = (f32[32,256]{1,0:T(8,128)}, f32[32,256]{1,0:T(8,128)S(1)}, u32[]{:S(2)}) copy-start(f32[32,256]{1,0:T(8,128)S(1)} %get-tuple-element.466) | copy-start | bytes 98308 | tf_op jit(solution)/shard_map/while
  393.8 12.5 %copy-start.6 = (f32[32,256]{1,0:T(8,128)}, f32[32,256]{1,0:T(8,128)S(1)}, u32[]{:S(2)}) copy-start(f32[32,256]{1,0:T(8,128)S(1)} %get-tuple-element.466) | copy-start | bytes 98308 | tf_op jit(solution)/shard_map/while
  393.8 12.5 %copy-start.9 = (s32[256]{0:T(256)S(1)}, s32[256]{0:T(256)}, u32[]{:S(2)}) copy-start(s32[256]{0:T(256)} %copy-done.8) | copy-start | bytes 3076 | tf_op jit(solution)/shard_map/while
  393.8 12.5 %copy-start.11 = (s32[256]{0:T(256)S(1)}, s32[256]{0:T(256)}, u32[]{:S(2)}) copy-start(s32[256]{0:T(256)} %copy-done.10) | copy-start | bytes 3076 | tf_op jit(solution)/shard_map/while
  393.8 12.5 %copy-start.14 = (s32[1,16]{1,0:T(1,128)S(1)}, s32[1,16]{1,0:T(1,128)}, u32[]{:S(2)}) copy-start(s32[1,16]{1,0:T(1,128)} %get-tuple-element.514) | copy-start | bytes 196 | tf_op jit(solution)/shard_map/while
  393.8 12.5 %copy-start.17 = (s32[4]{0:T(128)S(1)}, s32[4]{0:T(128)}, u32[]{:S(2)}) copy-start(s32[4]{0:T(128)} %copy-done.16) | copy-start | bytes 52 | tf_op jit(solution)/shard_map/while
  445.2 12.5 %copy-start.6 = (f32[32,256]{1,0:T(8,128)}, f32[32,256]{1,0:T(8,128)S(1)}, u32[]{:S(2)}) copy-start(f32[32,256]{1,0:T(8,128)S(1)} %get-tuple-element.466) | copy-start | bytes 98308 | tf_op jit(solution)/shard_map/while
  445.2 12.5 %copy-start.9 = (s32[256]{0:T(256)S(1)}, s32[256]{0:T(256)}, u32[]{:S(2)}) copy-start(s32[256]{0:T(256)} %copy-done.8) | copy-start | bytes 3076 | tf_op jit(solution)/shard_map/while
  445.3 12.5 %copy-start.11 = (s32[256]{0:T(256)S(1)}, s32[256]{0:T(256)}, u32[]{:S(2)}) copy-start(s32[256]{0:T(256)} %copy-done.10) | copy-start | bytes 3076 | tf_op jit(solution)/shard_map/while
  445.3 12.5 %copy-start.14 = (s32[1,16]{1,0:T(1,128)S(1)}, s32[1,16]{1,0:T(1,128)}, u32[]{:S(2)}) copy-start(s32[1,16]{1,0:T(1,128)} %get-tuple-element.514) | copy-start | bytes 196 | tf_op jit(solution)/shard_map/while
  445.3 12.5 %copy-start.17 = (s32[4]{0:T(128)S(1)}, s32[4]{0:T(128)}, u32[]{:S(2)}) copy-start(s32[4]{0:T(128)} %copy-done.16) | copy-start | bytes 52 | tf_op jit(solution)/shard_map/while
  496.7 12.5 %copy-start.6 = (f32[32,256]{1,0:T(8,128)}, f32[32,256]{1,0:T(8,128)S(1)}, u32[]{:S(2)}) copy-start(f32[32,256]{1,0:T(8,128)S(1)} %get-tuple-element.466) | copy-start | bytes 98308 | tf_op jit(solution)/shard_map/while
  496.7 12.5 %copy-start.9 = (s32[256]{0:T(256)S(1)}, s32[256]{0:T(256)}, u32[]{:S(2)}) copy-start(s32[256]{0:T(256)} %copy-done.8) | copy-start | bytes 3076 | tf_op jit(solution)/shard_map/while
  496.7 12.5 %copy-start.11 = (s32[256]{0:T(256)S(1)}, s32[256]{0:T(256)}, u32[]{:S(2)}) copy-start(s32[256]{0:T(256)} %copy-done.10) | copy-start | bytes 3076 | tf_op jit(solution)/shard_map/while
  496.7 12.5 %copy-start.14 = (s32[1,16]{1,0:T(1,128)S(1)}, s32[1,16]{1,0:T(1,128)}, u32[]{:S(2)}) copy-start(s32[1,16]{1,0:T(1,128)} %get-tuple-element.514) | copy-start | bytes 196 | tf_op jit(solution)/shard_map/while
  496.7 12.5 %copy-start.17 = (s32[4]{0:T(128)S(1)}, s32[4]{0:T(128)}, u32[]{:S(2)}) copy-start(s32[4]{0:T(128)} %copy-done.16) | copy-start | bytes 52 | tf_op jit(solution)/shard_map/while
  512.3 32.3 %copy-start.4 = (bf16[64,4096]{1,0:T(8,128)(2,1)S(1)}, bf16[64,4096]{1,0:T(8,128)(2,1)}, u32[]{:S(2)}) copy-start(bf16[64,4096]{1,0:T(8,128)(2,1)} %param.14) | copy-start | bytes 1572868
  512.4 33.1 %copy-start.2 = (bf16[192,6144]{1,0:T(8,128)(2,1)S(1)}, bf16[192,6144]{1,0:T(8,128)(2,1)}, u32[]{:S(2)}) copy-start(bf16[192,6144]{1,0:T(8,128)(2,1)} %param.13) | copy-start | bytes 7077892
  (31 other events, 241.2 us)
Sparse Core Ops, SparseCore 0:
  9.6 168.9 all-gather.9
  180.3 29.9 all-gather.13
  211.8 45.0 all-gather.11
  258.4 45.6 all-gather.7
where the time goes:
time: 564 us; the launch traced here: 554 us
  waiting for transfers between devices  230 us (41%)
  matrix products  159 us (28%)
  blocking collectives  68.2 us (12%)
  other arithmetic  48.7 us (9%)
  local copies, waits for them, and re-layouts  29.8 us (5%)
  between operations  14 us (2%)
    all_gather x1, waiting for transfers between devices, on_device(): lax.all_gather(w_uq, 'seq', axis=0, tiled=True)  123 us
    dot_general x4, matrix products, block_step(): jnp.einsum('hqk,khv->hqv', weights.astype(jnp.bfloat16), value_block, pre...  49 us
    all_gather x1, waiting for transfers between devices, on_device(): lax.all_gather(w_uk, 'seq', axis=0, tiled=True)  47.2 us
    all_gather x1, waiting for transfers between devices, on_device(): lax.all_gather(w_uv, 'seq', axis=0, tiled=True)  46.7 us
    dot_general x4, matrix products, block_step(): jnp.einsum('hqr,kr->hqk', query_rope, rope_block, preferred_element_type=...  42 us
    reduce_sum x4, other arithmetic, block_step(): new_total = run_total * shrink + jnp.sum(weights, axis=2)  34.8 us
    dot_general x4, matrix products, slice_latent(): jnp.dot(latent_block, rows_uv, preferred_element_type=jnp.float32)  27.4 us
    all_gather x1, blocking collectives, on_device(): lax.all_gather(key_rope, 'seq', axis=0, tiled=True)  25 us
  transfers between devices with their start and end apart: 4, of which 4 were waited for; matrix products, arithmetic and copies ran while one was open for 4% of the time, Pallas kernels for 0%

commit v1 on v0

--- a/solution.py
+++ b/solution.py
@@ -1,8 +1,11 @@
+import functools
 import math
 
 import jax
 import jax.numpy as jnp
 from jax import lax
+from jax.experimental import pallas as pl
+from jax.experimental.pallas import tpu as pltpu
 from jax.sharding import PartitionSpec as P
 
 NOPE = 128
@@ -38,7 +41,7 @@
     return base * half_block + index % half_block
 
 
-def on_device(query_latent, key_latent, rope_key, w_uq, w_uk, w_uv, block_order, segment_ids):
+def by_tokens(query_latent, key_latent, rope_key, w_uq, w_uk, w_uv, block_order, segment_ids):
     query_local, key_local = (
         lax.all_gather(query_latent[0], "tp", axis=1, tiled=True),
         lax.all_gather(key_latent[0], "tp", axis=1, tiled=True),
@@ -143,6 +146,213 @@
     return (context, clipped_uq, clipped_uk)
 
 
+def turned(values, cosine, sine):
+    half = values.shape[-1] // 2
+    swapped = jnp.concatenate([values[:, half:], values[:, :half]], axis=1)
+    return values * cosine + swapped * sine
+
+
+def attend(
+    block, tile, own, order, first_chunk, stored_at,
+    query_ref, key_ref, rope_ref, wq_ref, wk_ref, wv_ref, cos_ref, sin_ref, col_ref, row_ref,
+    context_ref, peak_ref,
+    q_s, k_s, v_s, s_s, m_s,
+):
+    count = query_ref.shape[0]
+    scale = 1.0 / math.sqrt(NOPE + ROPE)
+    width = NOPE + ROPE
+    rows = min(count, 4 * block)
+
+    def project(step, unused):
+        at = pl.multiple_of(step * rows, rows)
+        latent = key_ref[pl.ds(at, rows), :]
+        nope = jnp.dot(latent, wk_ref[...], preferred_element_type=jnp.float32).astype(jnp.bfloat16)
+        value = jnp.dot(latent, wv_ref[...], preferred_element_type=jnp.float32).astype(jnp.bfloat16)
+        full = jnp.dot(
+            query_ref[pl.ds(at, rows), :], wq_ref[...], preferred_element_type=jnp.float32
+        )
+        for part in range(rows // block):
+            lo, hi = part * block, (part + 1) * block
+            to = pl.multiple_of(order[step * (rows // block) + part] * block, block)
+            there = pl.ds(to, block)
+            cosine, sine = cos_ref[there, :], sin_ref[there, :]
+            raw = rope_ref[pl.ds(pl.multiple_of(at + lo, block), block), :].astype(jnp.float32)
+            key_rope = turned(raw, cosine, sine).astype(jnp.bfloat16)
+            v_s[there, :] = value[lo:hi, :]
+            for head in range(own):
+                base = head * width
+                k_s[head, there, :NOPE] = nope[lo:hi, head * NOPE : (head + 1) * NOPE]
+                k_s[head, there, NOPE:] = key_rope
+                q_s[head, there, :NOPE] = full[lo:hi, base : base + NOPE].astype(jnp.bfloat16)
+                q_s[head, there, NOPE:] = turned(
+                    full[lo:hi, base + NOPE : base + width], cosine, sine
+                ).astype(jnp.bfloat16)
+        return unused
+
+    lax.fori_loop(0, count // rows, project, 0)
+
+    def per_tile(number, best):
+        first = first_chunk[number]
+        here = pl.ds(pl.multiple_of(number * tile, tile), tile)
+        for head in range(own):
+            m_s[head] = jnp.full((tile, 128), masked_value, jnp.float32)
+
+        def score(chunk, unused):
+            there = pl.ds(pl.multiple_of(chunk * tile, tile), tile)
+            gap = (chunk - number) * tile
+            later = lax.broadcasted_iota(jnp.int32, (tile, tile), 1) + gap
+            now = lax.broadcasted_iota(jnp.int32, (tile, tile), 0)
+            allowed = (later <= now) & (col_ref[here, :] == row_ref[chunk])
+            for head in range(own):
+                raw = lax.dot_general(
+                    q_s[head, here, :], k_s[head, there, :], (((1,), (1,)), ((), ())),
+                    preferred_element_type=jnp.float32,
+                )
+                raw = jnp.where(allowed, raw, masked_value)
+                s_s[chunk - first, head] = raw
+                best_here = m_s[head]
+                for lane in range(tile // 128):
+                    best_here = jnp.maximum(best_here, raw[:, lane * 128 : (lane + 1) * 128])
+                m_s[head] = best_here
+            return unused
+
+        lax.fori_loop(first, number + 1, score, 0)
+        tops = []
+        for head in range(own):
+            top = jnp.max(m_s[head], axis=1, keepdims=True)
+            m_s[head] = jnp.broadcast_to(top, (tile, 128))
+            tops.append(jnp.broadcast_to(jnp.max(top, axis=0, keepdims=True), (1, 128)))
+
+        factor = scale * math.log2(math.e)
+
+        def mix(chunk, state):
+            there = pl.ds(pl.multiple_of(chunk * tile, tile), tile)
+            out = []
+            for head in range(own):
+                total, mixed = state[head]
+                top = m_s[head]
+                raw = s_s[chunk - first, head]
+                pieces = [
+                    jnp.exp2((raw[:, lane * 128 : (lane + 1) * 128] - top) * factor)
+                    for lane in range(tile // 128)
+                ]
+                for piece in pieces:
+                    total = total + piece
+                weights = jnp.concatenate([piece.astype(jnp.bfloat16) for piece in pieces], axis=1)
+                mixed = mixed + jnp.dot(
+                    weights, v_s[there, head * VD : (head + 1) * VD],
+                    preferred_element_type=jnp.float32,
+                )
+                out.append((total, mixed))
+            return tuple(out)
+
+        zero = tuple(
+            (jnp.zeros((tile, 128), jnp.float32), jnp.zeros((tile, VD), jnp.float32))
+            for head in range(own)
+        )
+        state = lax.fori_loop(first, number + 1, mix, zero)
+        for head in range(own):
+            total, mixed = state[head]
+            done = (mixed / jnp.sum(total, axis=1, keepdims=True)).astype(jnp.bfloat16)
+            for part in range(tile // block):
+                to = pl.multiple_of(stored_at[number * (tile // block) + part] * block, block)
+                context_ref[pl.ds(to, block), head * VD : (head + 1) * VD] = done[
+                    part * block : (part + 1) * block, :
+                ]
+        return jnp.maximum(best, jnp.concatenate(tops, axis=0))
+
+    best = lax.fori_loop(
+        0, count // tile, per_tile, jnp.full((own, 128), masked_value, jnp.float32)
+    )
+    peak_ref[...] = best * scale
+
+
+def by_heads(query_latent, key_latent, rope_key, w_uq, w_uk, w_uv, block_order, segment_ids):
+    devices = lax.axis_size("seq")
+    heads = w_uq.shape[1] // (NOPE + ROPE)
+    own = heads // devices
+    swap = functools.partial(
+        lax.all_to_all, axis_name="seq", split_axis=1, concat_axis=0, tiled=True
+    )
+    wq, wk, wv = swap(w_uq), swap(w_uk), swap(w_uv)
+
+    def everywhere(latent):
+        return lax.all_gather(
+            lax.all_gather(latent, "tp", axis=1, tiled=True), "seq", axis=0, tiled=True
+        )
+
+    query, key = everywhere(query_latent[0]), everywhere(key_latent[0])
+    rope = lax.all_gather(rope_key[0], "seq", axis=0, tiled=True)
+    order, labels = block_order[0], segment_ids[0]
+    count, blocks = labels.shape[0], order.shape[0]
+    block = count // blocks
+    tile = 2 * block
+    chunks = count // tile
+    cosine, sine = turning(jnp.arange(count, dtype=jnp.int32), ROPE)
+    cosine = jnp.concatenate([cosine, cosine], axis=1)
+    sine = jnp.concatenate([-sine, sine], axis=1)
+    stored_at = jnp.argmax(
+        order[None, :] == jnp.arange(blocks, dtype=jnp.int32)[:, None], axis=1
+    ).astype(jnp.int32)
+    heads_of = labels[::tile]
+    first_chunk = (
+        jnp.sum((labels[None, :] < heads_of[:, None]).astype(jnp.int32), axis=1) // tile
+    ).astype(jnp.int32)
+    vmem = pl.BlockSpec(memory_space=pltpu.VMEM)
+    smem = pl.BlockSpec(memory_space=pltpu.SMEM)
+    context, peak = pl.pallas_call(
+        functools.partial(attend, block, tile, own),
+        out_shape=(
+            jax.ShapeDtypeStruct((count, own * VD), jnp.bfloat16),
+            jax.ShapeDtypeStruct((own, 128), jnp.float32),
+        ),
+        in_specs=[smem] * 3 + [vmem] * 10,
+        out_specs=(vmem, vmem),
+        scratch_shapes=[
+            pltpu.VMEM((own, count, NOPE + ROPE), jnp.bfloat16),
+            pltpu.VMEM((own, count, NOPE + ROPE), jnp.bfloat16),
+            pltpu.VMEM((count, own * VD), jnp.bfloat16),
+            pltpu.VMEM((chunks, own, tile, tile), jnp.float32),
+            pltpu.VMEM((own, tile, 128), jnp.float32),
+        ],
+        compiler_params=pltpu.CompilerParams(vmem_limit_bytes=60 * 1024 * 1024),
+        cost_estimate=pl.CostEstimate(
+            flops=12_000_000_000, bytes_accessed=16_000_000, transcendentals=4_000_000
+        ),
+        name="attend",
+    )(
+        order, first_chunk, stored_at, query, key, rope, wq, wk, wv, cosine, sine,
+        labels[:, None], labels.reshape(chunks, 1, tile),
+    )
+    context = lax.all_to_all(context, "seq", split_axis=0, concat_axis=1, tiled=True)[None]
+    mine = lax.dynamic_update_slice(
+        jnp.full((heads,), masked_value, jnp.float32), peak[:, 0], (lax.axis_index("seq") * own,)
+    )
+    return (context,) + clipped(w_uq, w_uk, lax.pmax(mine, ("seq", "dp")), heads)
+
+
+def clipped(w_uq, w_uk, head_max, heads):
+    ratio = CLIP / jnp.maximum(head_max, CLIP)
+    root = jnp.sqrt(ratio)
+    factors = jnp.concatenate(
+        [
+            jnp.broadcast_to(root[:, None], (heads, NOPE)),
+            jnp.broadcast_to(ratio[:, None], (heads, ROPE)),
+        ],
+        axis=1,
+    ).reshape(heads * (NOPE + ROPE))
+    clipped_uq = (w_uq.astype(jnp.float32) * factors[None, :]).astype(jnp.bfloat16)
+    clipped_uk = (w_uk.astype(jnp.float32) * jnp.repeat(root, NOPE)[None, :]).astype(jnp.bfloat16)
+    return (clipped_uq, clipped_uk)
+
+
+def on_device(*arrays):
+    heads = arrays[3].shape[1] // (NOPE + ROPE)
+    if heads % (2 * lax.axis_size("seq")) == 0:
+        return by_heads(*arrays)
+    return by_tokens(*arrays)
+
+
 def solution(mesh):
     placed = (
         P("dp", "seq", "tp"),

time: 564 us -> 318 us (0.56); the launches traced: 554 us -> 317 us
  waiting for transfers between devices: 230 us -> 40.5 us
  matrix products: 159 us -> 0 us
  blocking collectives: 68.2 us -> 175 us
  Pallas kernels: 0 us -> 40.5 us
  other arithmetic: 48.7 us -> 9.9 us
  starting transfers between devices: 0.16 us -> 26.8 us
  local copies, waits for them, and re-layouts: 29.8 us -> 10.7 us
    all_gather x4 -> x2, waiting for transfers between devices: 228 us -> 0.01 us  [everywhere(): lax.all_gather(lax.all_gather(latent, 'tp', axis=1, tiled=True), 'seq', a...]
    dot_general x21 -> x0, matrix products: 159 us -> none  [the longest x4 49 us: block_step(): jnp.einsum('hqk,khv->hqv', weights.astype(jnp.bfloat16), value_block, pre...]
    all_gather x3, blocking collectives: 43.2 us -> 110 us  [the longest x1 91.7 us: by_heads(): rope = lax.all_gather(rope_key[0], 'seq', axis=0, tiled=True)]
    pallas_call x0 -> x1, Pallas kernels: none -> 40.5 us  [by_heads(): pl.pallas_call(functools.partial(attend, block, tile, own), out_shape=(ja...]
    all_to_all x0 -> x4, waiting for transfers between devices: none -> 40.5 us  [the longest x3 40.5 us: by_heads(): wq, wk, wv = (swap(w_uq), swap(w_uk), swap(w_uv))]
    pmax x1, blocking collectives: 25 us -> 64.5 us  [by_heads(): lax.pmax(mine, ('seq', 'dp'))]
    reduce_sum x9 -> x1, other arithmetic: 35.9 us -> 0.2 us  [by_heads(): jnp.sum((labels[None, :] < heads_of[:, None]).astype(jnp.int32), axis=1)]
    all_to_all x0 -> x4, starting transfers between devices: none -> 26.7 us  [the longest x3 21.4 us: by_heads(): wq, wk, wv = (swap(w_uq), swap(w_uk), swap(w_uv))]
  transfers between devices with their start and end apart: 4 -> 6, of which waited for: 4 -> 2; matrix products, arithmetic and copies ran while one was open for 4% -> 5% of each run, Pallas kernels for 0% -> 0%
where the time goes in v1:
time: 318 us; the launch traced here: 317 us
  blocking collectives  175 us (55%)
  waiting for transfers between devices  40.5 us (13%)
  Pallas kernels  40.5 us (13%)
  starting transfers between devices  26.8 us (8%)
  between operations  14.1 us (4%)
  local copies, waits for them, and re-layouts  10.7 us (3%)
  other arithmetic  9.9 us (3%)
    all_gather x1, blocking collectives, by_heads(): rope = lax.all_gather(rope_key[0], 'seq', axis=0, tiled=True)  91.7 us
    pmax x1, blocking collectives, by_heads(): lax.pmax(mine, ('seq', 'dp'))  64.5 us
    pallas_call x1, Pallas kernels, by_heads(): pl.pallas_call(functools.partial(attend, block, tile, own), out_shape=(ja...  40.5 us
    all_to_all x3, waiting for transfers between devices, by_heads(): wq, wk, wv = (swap(w_uq), swap(w_uk), swap(w_uv))  40.5 us
    all_to_all x3, starting transfers between devices, by_heads(): wq, wk, wv = (swap(w_uq), swap(w_uk), swap(w_uv))  21.4 us
    all_gather x2, blocking collectives, everywhere(): lax.all_gather(latent, 'tp', axis=1, tiled=True)  18.3 us
  transfers between devices with their start and end apart: 6, of which 2 were waited for; matrix products, arithmetic and copies ran while one was open for 5% of the time, Pallas kernels for 0%

profile of v1, /device:TPU:9, one launch (start us, length us, event | category | flops | bytes accessed | tf_op | source)
XLA Modules:
  0.0 317.0 jit_solution(16420558451450487320)
XLA Ops:
  7.2 7.1 %all-gather.2 = bf16[1,256,512]{2,1,0:T(8,128)(2,1)} all-gather(bf16[1,256,256]{2,1,0:T(8,128)(2,1)} %param.9), channel_id=4, replica_groups=mesh['seq'=8,'tp'=2,'dp'=2] {'tp'}, dimensions={2}, use_global_device_ids=true | all-gather | bytes 393216 | tf_op jit(solution)/shard_map/all_gather | solution.py:281
  14.4 11.2 %all-gather = bf16[1,256,1536]{2,1,0:T(8,128)(2,1)} all-gather(bf16[1,256,768]{2,1,0:T(8,128)(2,1)} %param.8), channel_id=2, replica_groups=mesh['seq'=8,'tp'=2,'dp'=2] {'tp'}, dimensions={2}, use_global_device_ids=true | all-gather | bytes 1179648 | tf_op jit(solution)/shard_map/all_gather | solution.py:281
  25.6 0.8 copy.42
  26.5 6.9 %all-to-all-start.2 = ((bf16[64,8,512]{2,0,1:T(8,128)(2,1)}), bf16[64,8,512]{2,0,1:T(8,128)(2,1)S(1)}, u32[]{:S(2)}, u32[]{:S(2)}) async-start(bf16[64,8,512]{2,0,1:T(8,128)(2,1)} %bitcast.30), calls=%async_computation.2 | async-start | bytes 1048576 | tf_op jit(solution)/shard_map/all_to_all | solution.py:277
  33.4 0.8 copy.43
  34.2 17.6 %all-to-all-done.2 = bf16[64,8,512]{2,0,1:T(8,128)(2,1)S(1)} async-done(((bf16[64,8,512]{2,0,1:T(8,128)(2,1)}), bf16[64,8,512]{2,0,1:T(8,128)(2,1)S(1)}, u32[]{:S(2)}, u32[]{:S(2)}) %all-to-all-start.2) | async-done | bytes 524320 | tf_op jit(solution)/shard_map/all_to_all | solution.py:277
  51.8 7.7 %all-to-all-start.1 = ((bf16[64,8,512]{2,0,1:T(8,128)(2,1)}), bf16[64,8,512]{2,0,1:T(8,128)(2,1)}, u32[]{:S(2)}, u32[]{:S(2)}) async-start(bf16[64,8,512]{2,0,1:T(8,128)(2,1)} %bitcast.31), calls=%async_computation.1 | async-start | bytes 1048576 | tf_op jit(solution)/shard_map/all_to_all | solution.py:277
  59.5 1.6 copy.41
  61.1 22.8 %all-to-all-done.1 = bf16[64,8,512]{2,0,1:T(8,128)(2,1)} async-done(((bf16[64,8,512]{2,0,1:T(8,128)(2,1)}), bf16[64,8,512]{2,0,1:T(8,128)(2,1)}, u32[]{:S(2)}, u32[]{:S(2)}) %all-to-all-start.1) | async-done | bytes 524320 | tf_op jit(solution)/shard_map/all_to_all | solution.py:277
  83.9 6.8 %all-to-all-start = ((bf16[192,8,768]{2,0,1:T(8,128)(2,1)}), bf16[192,8,768]{2,0,1:T(8,128)(2,1)}, u32[]{:S(2)}, u32[]{:S(2)}) async-start(bf16[192,8,768]{2,0,1:T(8,128)(2,1)} %bitcast.33), calls=%async_computation | async-start | bytes 4718592 | tf_op jit(solution)/shard_map/all_to_all | solution.py:277
  90.8 1.4 copy.33.col_ref
  92.6 91.7 %all-gather.4 = bf16[1,2048,64]{2,1,0:T(8,128)(2,1)} all-gather(bf16[1,256,64]{2,1,0:T(8,128)(2,1)S(1)} %copy.28), channel_id=6, replica_groups=mesh['seq'=8,'tp'=2,'dp'=2] {'seq'}, dimensions={1}, use_global_device_ids=true | all-gather | bytes 294912 | tf_op jit(solution)/shard_map/all_gather | solution.py:285
  184.2 0.6 and_select_fusion.first_chunk
  184.8 0.7 iota_reduce_fusion
  185.5 3.7 %fusion = (f32[2048,32]{1,0:T(8,128)S(1)}, f32[2048,32]{1,0:T(8,128)S(1)}, f32[2048,32]{1,0:T(8,128)S(1)}) fusion(f32[32]{0:T(128)S(1)} %multiply_exponential_fusion, f32[2048]{0:T(1024)S(1)} %iota_convert_fusion), kind=kLoop, calls=%fused_computation.9 | loop fusion | flops 131072 | bytes 794752 | tf_op jit(solution)/shard_map/neg | solution.py:293
  189.2 1.9 pad_maximum_fusion
  191.2 40.5 %attend.1 = (bf16[2048,512]{1,0:T(8,128)(2,1)}, f32[4,128]{1,0:T(4,128)}) custom-call(s32[16]{0:T(128)} %bitcast.45, s32[8]{0:T(128)} %and_select_fusion.first_chunk, s32[16]{0:T(128)} %get-tuple-element.6.stored_at, bf16[2048,1536]{1,0:T(8,128)(2,1)} %bitcast.43, bf16[2048,512]{1,0:T(8,128)(2,1)} %bitcast.44, bf16[2048,64]{1,0:T(8,128)(2,1)} %bitcast.36, ...), custom_call_target="tpu_custom_call" | custom-call | flops 12000000000 | bytes 16000000 | tf_op jit(solution)/shard_map/attend/pallas_call | solution.py:303
  231.7 5.4 %all-to-all-start.3 = ((bf16[8,256,512]{2,1,0:T(8,128)(2,1)}), bf16[8,256,512]{2,1,0:T(8,128)(2,1)}, u32[]{:S(2)}, u32[]{:S(2)}) async-start(bf16[8,256,512]{2,1,0:T(8,128)(2,1)} %bitcast.34), calls=%async_computation.3 | async-start | bytes 4194304 | tf_op jit(solution)/shard_map/all_to_all | solution.py:327
  237.2 0.2 dynamic_update_slice.3
  237.4 64.5 %pmax.7 = f32[32]{0:T(128)S(1)} all-reduce(f32[32]{0:T(128)S(1)} %dynamic_update_slice.3), channel_id=1, replica_groups=mesh['seq'=8,'tp'=2,'dp'=2] {'seq','dp'}, use_global_device_ids=true, to_apply=%region_2.3 | all-reduce | flops 32 | bytes 256 | tf_op jit(solution)/shard_map/pmax | solution.py:331
  302.3 0.9 multiply_convert_fusion.1
  303.2 1.9 multiply_convert_fusion
  305.0 2.8 copy.34
  307.8 2.3 broadcast_in_dim.8
  (37 shorter events, 1.0 us)
Async XLA Ops:
  7.2 18.5 %copy-start.2 = (bf16[64,4096]{1,0:T(8,128)(2,1)S(1)}, bf16[64,4096]{1,0:T(8,128)(2,1)}, u32[]{:S(2)}) copy-start(bf16[64,4096]{1,0:T(8,128)(2,1)} %param.13) | copy-start | bytes 1572868
  7.2 26.2 %copy-start.1 = (bf16[64,4096]{1,0:T(8,128)(2,1)S(1)}, bf16[64,4096]{1,0:T(8,128)(2,1)}, u32[]{:S(2)}) copy-start(bf16[64,4096]{1,0:T(8,128)(2,1)} %param.12) | copy-start | bytes 1572868
  7.2 184.0 %all-gather.10.cloned.1.call-start = ((), (), s32[]{:S(2)}) async-start(), calls=%async_computation.5 | async-start | bytes 2359296 | tf_op jit(solution)/shard_map/all_gather | solution.py:280
  14.4 176.8 %all-gather.8.cloned.1.call-start = ((), (), s32[]{:S(2)}) async-start(), calls=%async_computation.4 | async-start | bytes 7077888 | tf_op jit(solution)/shard_map/all_gather | solution.py:280
  25.6 33.9 %copy-start = (bf16[192,6144]{1,0:T(8,128)(2,1)S(1)}, bf16[192,6144]{1,0:T(8,128)(2,1)}, u32[]{:S(2)}) copy-start(bf16[192,6144]{1,0:T(8,128)(2,1)} %param.11) | copy-start | bytes 7077892
  26.5 25.3 %all-to-all-start.2 = ((bf16[64,8,512]{2,0,1:T(8,128)(2,1)}), bf16[64,8,512]{2,0,1:T(8,128)(2,1)S(1)}, u32[]{:S(2)}, u32[]{:S(2)}) async-start(bf16[64,8,512]{2,0,1:T(8,128)(2,1)} %bitcast.30), calls=%async_computation.2 | async-start | bytes 1048576 | tf_op jit(solution)/shard_map/all_to_all | solution.py:277
  51.8 9.3 %copy-start.3 = (bf16[64,8,512]{2,0,1:T(8,128)(2,1)}, bf16[64,8,512]{2,0,1:T(8,128)(2,1)S(1)}, u32[]{:S(2)}) copy-start(bf16[64,8,512]{2,0,1:T(8,128)(2,1)S(1)} %all-to-all-done.2) | copy-start | bytes 1572868
  51.8 32.1 %all-to-all-start.1 = ((bf16[64,8,512]{2,0,1:T(8,128)(2,1)}), bf16[64,8,512]{2,0,1:T(8,128)(2,1)}, u32[]{:S(2)}, u32[]{:S(2)}) async-start(bf16[64,8,512]{2,0,1:T(8,128)(2,1)} %bitcast.31), calls=%async_computation.1 | async-start | bytes 1048576 | tf_op jit(solution)/shard_map/all_to_all | solution.py:277
  83.9 6.8 %copy-start.4 = (s32[1,2048]{1,0:T(1,128)S(1)}, s32[1,2048]{1,0:T(1,128)}, u32[]{:S(2)}) copy-start(s32[1,2048]{1,0:T(1,128)} %param.15) | copy-start | bytes 24580
  83.9 8.3 %copy-start.5 = (bf16[1,256,64]{1,2,0:T(8,128)(2,1)S(1)}, bf16[1,256,64]{1,2,0:T(8,128)(2,1)}, u32[]{:S(2)}) copy-start(bf16[1,256,64]{1,2,0:T(8,128)(2,1)} %param.10) | copy-start | bytes 98308
  83.9 100.9 %copy-start.7 = (s32[1,16]{1,0:T(1,128)S(1)}, s32[1,16]{1,0:T(1,128)}, u32[]{:S(2)}) copy-start(s32[1,16]{1,0:T(1,128)} %param.14) | copy-start | bytes 196
  83.9 107.3 %all-to-all-start = ((bf16[192,8,768]{2,0,1:T(8,128)(2,1)}), bf16[192,8,768]{2,0,1:T(8,128)(2,1)}, u32[]{:S(2)}, u32[]{:S(2)}) async-start(bf16[192,8,768]{2,0,1:T(8,128)(2,1)} %bitcast.33), calls=%async_computation | async-start | bytes 4718592 | tf_op jit(solution)/shard_map/all_to_all | solution.py:277
  231.7 5.4 %copy-start.6 = (f32[4,128]{1,0:T(4,128)S(1)}, f32[4,128]{1,0:T(4,128)}, u32[]{:S(2)}) copy-start(f32[4,128]{1,0:T(4,128)} %get-tuple-element.8) | copy-start | bytes 6148
  231.7 73.3 %all-to-all-start.3 = ((bf16[8,256,512]{2,1,0:T(8,128)(2,1)}), bf16[8,256,512]{2,1,0:T(8,128)(2,1)}, u32[]{:S(2)}, u32[]{:S(2)}) async-start(bf16[8,256,512]{2,1,0:T(8,128)(2,1)} %bitcast.34), calls=%async_computation.3 | async-start | bytes 4194304 | tf_op jit(solution)/shard_map/all_to_all | solution.py:327
Sparse Core Ops, SparseCore 0:
  14.5 36.2 all-gather.9
  52.4 113.5 all-gather.7

commit v2 on v1

--- a/solution.py
+++ b/solution.py
@@ -267,22 +267,221 @@
     peak_ref[...] = best * scale
 
 
+MESH = pl.DeviceIdType.MESH
+
+
+def window(start, size):
+    return pl.ds(pl.multiple_of(start * size, size), size)
+
+
+def greet(wheres):
+    barrier = pltpu.get_barrier_semaphore()
+    for where in wheres:
+        pl.semaphore_signal(barrier, inc=1, device_id=where, device_id_type=MESH)
+    pl.semaphore_wait(barrier, len(wheres))
+
+
+def spread(
+    n, query_ref, key_ref, rope_ref, uq_ref, uk_ref, uv_ref,
+    query_out, key_out, rope_out, wq_out, wk_out, wv_out,
+    sends, got_query, got_key, got_rope, got_weight, local,
+):
+    s, t, d = lax.axis_index("seq"), lax.axis_index("tp"), lax.axis_index("dp")
+    partner = s + 1 - 2 * lax.rem(s, 2)
+    near = sorted(range(1, n // 2), key=lambda k: (min(k, n // 2 - k), k))
+    same = lambda k: lax.rem(s + 2 * k, n)
+    cross = lambda k: lax.rem(partner + 2 * k, n)
+    beside, across, mate = {"tp": 1 - t}, {"dp": 1 - d}, {"seq": partner}
+    greet(
+        [mate, beside, across]
+        + [{"seq": same(k)} for k in near]
+        + [{"seq": cross(k)} for k in near]
+    )
+    rows, wide = query_ref.shape
+    thin = key_ref.shape[1]
+    weights = ((uq_ref, wq_out), (uk_ref, wk_out), (uv_ref, wv_out))
+    started = []
+
+    def link(source, target, arrived, where, sender):
+        return pltpu.make_async_remote_copy(
+            src_ref=source, dst_ref=target, send_sem=sends.at[sender], recv_sem=arrived,
+            device_id=where, device_id_type=MESH,
+        )
+
+    def send(source, target, arrived, where):
+        copy = link(source, target, arrived, where, len(started))
+        copy.start()
+        started.append(copy)
+
+    def arrive(target, arrived):
+        link(target, target, arrived, mate, 0).wait_recv()
+
+    def spots(src, tp):
+        return (
+            (query_out.at[window(src, rows), window(tp, wide)], got_query.at[src, tp]),
+            (key_out.at[window(src, rows), window(tp, thin)], got_key.at[src, tp]),
+        )
+
+    def rope_spot(src):
+        return (rope_out.at[window(src, rows), :], got_rope.at[src])
+
+    def own_latents(where, rope):
+        for source, (target, arrived) in zip((query_ref, key_ref), spots(s, t)):
+            send(source, target, arrived, where)
+        if rope:
+            send(rope_ref, *rope_spot(s), where)
+
+    def await_latents(src, tp, rope):
+        for target, arrived in spots(src, tp):
+            arrive(target, arrived)
+        if rope:
+            arrive(*rope_spot(src))
+
+    def pass_latents(src, tp, where, rope):
+        for target, arrived in spots(src, tp):
+            send(target, target, arrived, where)
+        if rope:
+            target, arrived = rope_spot(src)
+            send(target, target, arrived, where)
+
+    def weight_spot(index, src, half):
+        out = weights[index][1]
+        depth = weights[index][0].shape[0] // 2
+        return (out.at[window(src * 2 + half, depth), :], got_weight.at[index, src, half])
+
+    def own_weights(to):
+        for index, (ref, out) in enumerate(weights):
+            piece = ref.at[window(d, ref.shape[0] // 2), window(to, out.shape[1])]
+            send(piece, *weight_spot(index, s, d), {"seq": to})
+
+    def pass_weights(src):
+        for index in range(len(weights)):
+            target, arrived = weight_spot(index, src, d)
+            arrive(target, arrived)
+            send(target, target, arrived, across)
+
+    own_latents(beside, False)
+    for k in near:
+        own_latents({"seq": same(k)}, True)
+        own_weights(same(k))
+        own_weights(cross(k))
+    own_latents(mate, True)
+    own_weights(partner)
+    kept = [
+        pltpu.make_async_copy(source, target, local.at[place])
+        for place, (source, target) in enumerate(
+            [(query_ref, spots(s, t)[0][0]), (key_ref, spots(s, t)[1][0]), (rope_ref, rope_spot(s)[0])]
+            + [
+                (ref.at[:, window(s, out.shape[1])], out.at[window(s, ref.shape[0]), :])
+                for ref, out in weights
+            ]
+        )
+    ]
+    for copy in kept:
+        copy.start()
+    pass_weights(partner)
+    for k in near:
+        await_latents(same(k), t, True)
+        pass_latents(same(k), t, beside, False)
+        pass_latents(same(k), t, mate, True)
+        pass_weights(same(k))
+        pass_weights(cross(k))
+    for k in [0] + near:
+        await_latents(same(k), 1 - t, False)
+        pass_latents(same(k), 1 - t, mate, False)
+    for k in [0] + near:
+        await_latents(cross(k), t, True)
+        await_latents(cross(k), 1 - t, False)
+    for src in [partner] + [same(k) for k in near] + [cross(k) for k in near]:
+        for index in range(len(weights)):
+            arrive(*weight_spot(index, src, 1 - d))
+    for copy in started:
+        copy.wait_send()
+    for copy in kept:
+        copy.wait()
+
+
+def give_back(n, context_ref, peak_ref, out_ref, peaks_ref, sends, got_context, got_peak, local):
+    s, d = lax.axis_index("seq"), lax.axis_index("dp")
+    rows, wide = out_ref.shape[0], context_ref.shape[1]
+    steps = [k for k in range(1, n)]
+    peers = [lax.rem(s + k, n) for k in steps]
+    wheres = [{"seq": to} for to in peers]
+    others = [{"dp": 1 - d}] + [{"seq": to, "dp": 1 - d} for to in peers]
+    greet(wheres + others)
+    started = []
+
+    def link(source, target, arrived, where, sender):
+        return pltpu.make_async_remote_copy(
+            src_ref=source, dst_ref=target, send_sem=sends.at[sender], recv_sem=arrived,
+            device_id=where, device_id_type=MESH,
+        )
+
+    def send(source, target, arrived, where):
+        copy = link(source, target, arrived, where, len(started))
+        copy.start()
+        started.append(copy)
+
+    me = d * n + s
+    for where in wheres + others:
+        send(peak_ref, peaks_ref.at[me], got_peak.at[me], where)
+    for to, where in zip(peers, wheres):
+        send(context_ref.at[window(to, rows), :], out_ref.at[:, window(s, wide)], got_context.at[s], where)
+    kept = [
+        pltpu.make_async_copy(peak_ref, peaks_ref.at[me], local.at[0]),
+        pltpu.make_async_copy(context_ref.at[window(s, rows), :], out_ref.at[:, window(s, wide)], local.at[1]),
+    ]
+    for copy in kept:
+        copy.start()
+    for src in peers:
+        target = out_ref.at[:, window(src, wide)]
+        link(target, target, got_context.at[src], wheres[0], 0).wait_recv()
+    for src in [d * n + p for p in peers] + [(1 - d) * n + p for p in peers] + [(1 - d) * n + s]:
+        link(peaks_ref.at[src], peaks_ref.at[src], got_peak.at[src], wheres[0], 0).wait_recv()
+    for copy in started:
+        copy.wait_send()
+    for copy in kept:
+        copy.wait()
+
+
 def by_heads(query_latent, key_latent, rope_key, w_uq, w_uk, w_uv, block_order, segment_ids):
     devices = lax.axis_size("seq")
     heads = w_uq.shape[1] // (NOPE + ROPE)
     own = heads // devices
-    swap = functools.partial(
-        lax.all_to_all, axis_name="seq", split_axis=1, concat_axis=0, tiled=True
-    )
-    wq, wk, wv = swap(w_uq), swap(w_uk), swap(w_uv)
-
-    def everywhere(latent):
-        return lax.all_gather(
-            lax.all_gather(latent, "tp", axis=1, tiled=True), "seq", axis=0, tiled=True
-        )
-
-    query, key = everywhere(query_latent[0]), everywhere(key_latent[0])
-    rope = lax.all_gather(rope_key[0], "seq", axis=0, tiled=True)
+    anyplace = pl.BlockSpec(memory_space=pl.ANY)
+    vmem = pl.BlockSpec(memory_space=pltpu.VMEM)
+    smem = pl.BlockSpec(memory_space=pltpu.SMEM)
+    sides = lax.axis_size("tp")
+    rows = query_latent.shape[1]
+    shapes = (
+        (devices * rows, sides * query_latent.shape[2]),
+        (devices * rows, sides * key_latent.shape[2]),
+        (devices * rows, ROPE),
+        (devices * w_uq.shape[0], w_uq.shape[1] // devices),
+        (devices * w_uk.shape[0], w_uk.shape[1] // devices),
+        (devices * w_uv.shape[0], w_uv.shape[1] // devices),
+    )
+    half = devices // 2
+    copies = 10 * half + 6 * (half - 1) + 3 * half + 6 * (devices - 1)
+    query, key, rope, wq, wk, wv = pl.pallas_call(
+        functools.partial(spread, devices),
+        out_shape=[jax.ShapeDtypeStruct(shape, jnp.bfloat16) for shape in shapes],
+        in_specs=[anyplace] * 6,
+        out_specs=[anyplace] * 6,
+        scratch_shapes=[
+            pltpu.SemaphoreType.DMA((copies,)),
+            pltpu.SemaphoreType.DMA((devices, sides)),
+            pltpu.SemaphoreType.DMA((devices, sides)),
+            pltpu.SemaphoreType.DMA((devices,)),
+            pltpu.SemaphoreType.DMA((3, devices, 2)),
+            pltpu.SemaphoreType.DMA((6,)),
+        ],
+        compiler_params=pltpu.CompilerParams(collective_id=0, has_side_effects=True),
+        cost_estimate=pl.CostEstimate(
+            flops=30_000_000_000, bytes_accessed=16_000_000, transcendentals=0
+        ),
+        name="spread",
+    )(query_latent[0], key_latent[0], rope_key[0], w_uq, w_uk, w_uv)
     order, labels = block_order[0], segment_ids[0]
     count, blocks = labels.shape[0], order.shape[0]
     block = count // blocks
@@ -298,8 +497,6 @@
     first_chunk = (
         jnp.sum((labels[None, :] < heads_of[:, None]).astype(jnp.int32), axis=1) // tile
     ).astype(jnp.int32)
-    vmem = pl.BlockSpec(memory_space=pltpu.VMEM)
-    smem = pl.BlockSpec(memory_space=pltpu.SMEM)
     context, peak = pl.pallas_call(
         functools.partial(attend, block, tile, own),
         out_shape=(
@@ -324,11 +521,25 @@
         order, first_chunk, stored_at, query, key, rope, wq, wk, wv, cosine, sine,
         labels[:, None], labels.reshape(chunks, 1, tile),
     )
-    context = lax.all_to_all(context, "seq", split_axis=0, concat_axis=1, tiled=True)[None]
-    mine = lax.dynamic_update_slice(
-        jnp.full((heads,), masked_value, jnp.float32), peak[:, 0], (lax.axis_index("seq") * own,)
-    )
-    return (context,) + clipped(w_uq, w_uk, lax.pmax(mine, ("seq", "dp")), heads)
+    context, peaks = pl.pallas_call(
+        functools.partial(give_back, devices),
+        out_shape=[
+            jax.ShapeDtypeStruct((rows, heads * VD), jnp.bfloat16),
+            jax.ShapeDtypeStruct((2 * devices, own, 128), jnp.float32),
+        ],
+        in_specs=[anyplace, vmem],
+        out_specs=[anyplace, vmem],
+        scratch_shapes=[
+            pltpu.SemaphoreType.DMA((3 * devices,)),
+            pltpu.SemaphoreType.DMA((devices,)),
+            pltpu.SemaphoreType.DMA((2 * devices,)),
+            pltpu.SemaphoreType.DMA((2,)),
+        ],
+        compiler_params=pltpu.CompilerParams(collective_id=1, has_side_effects=True),
+        name="give_back",
+    )(context, peak)
+    head_max = jnp.max(peaks[:, :, 0].reshape(2, heads), axis=0)
+    return (context[None],) + clipped(w_uq, w_uk, head_max, heads)
 
 
 def clipped(w_uq, w_uk, head_max, heads):
@@ -348,7 +559,8 @@
 
 def on_device(*arrays):
     heads = arrays[3].shape[1] // (NOPE + ROPE)
-    if heads % (2 * lax.axis_size("seq")) == 0:
+    pairs = lax.axis_size("tp") == 2 and lax.axis_size("dp") == 2
+    if pairs and heads % (2 * lax.axis_size("seq")) == 0:
         return by_heads(*arrays)
     return by_tokens(*arrays)
 

time: 318 us -> 212 us (0.67)
  blocking collectives: 175 us -> 0 us
  Pallas kernels: 40.5 us -> 193 us
  waiting for transfers between devices: 40.5 us -> 0 us
  starting transfers between devices: 26.8 us -> 0 us
  between operations: 14.1 us -> 0.69 us
  local copies, waits for them, and re-layouts: 10.7 us -> 7 us
    pallas_call x0 -> x2, Pallas kernels: none -> 156 us  [the longest x1 92.2 us: by_heads(): pl.pallas_call(functools.partial(spread, devices), out_shape=[jax.ShapeDt...]
    all_gather x3 -> x0, blocking collectives: 110 us -> none  [the longest x1 91.7 us: by_heads(): rope = lax.all_gather(rope_key[0], 'seq', axis=0, tiled=True)]
    pmax x1 -> x0, blocking collectives: 64.5 us -> none  [by_heads(): lax.pmax(mine, ('seq', 'dp'))]
    all_to_all x4 -> x0, waiting for transfers between devices: 40.5 us -> none  [the longest x3 40.5 us: by_heads(): wq, wk, wv = (swap(w_uq), swap(w_uk), swap(w_uv))]
    all_to_all x4 -> x0, starting transfers between devices: 26.7 us -> none  [the longest x3 21.4 us: by_heads(): wq, wk, wv = (swap(w_uq), swap(w_uk), swap(w_uv))]
    all_to_all x4 -> x0, local copies, waits for them, and re-layouts: 6 us -> none  [the longest x3 3.25 us: by_heads(): wq, wk, wv = (swap(w_uq), swap(w_uk), swap(w_uv))]
  transfers between devices with their start and end apart: 6 -> 0, of which waited for: 2 -> 0; matrix products, arithmetic and copies ran while one was open for 5% -> 0% of each run, Pallas kernels for 0% -> 0%
where the time goes in v2:
time: 212 us
  Pallas kernels  193 us (91%)
  other arithmetic  11.3 us (5%)
  local copies, waits for them, and re-layouts  7 us (3%)
    pallas_call x1, Pallas kernels, by_heads(): pl.pallas_call(functools.partial(spread, devices), out_shape=[jax.ShapeDt...  92.2 us
    pallas_call x1, Pallas kernels, by_heads(): pl.pallas_call(functools.partial(give_back, devices), out_shape=[jax.Shap...  63.7 us
    pallas_call x1, Pallas kernels, by_heads(): pl.pallas_call(functools.partial(attend, block, tile, own), out_shape=(ja...  37.5 us

profile of v2, /device:TPU:9, one launch (start us, length us, event | category | flops | bytes accessed | tf_op | source)
XLA Modules:
  0.0 212.3 jit_solution(8698336569255931442)
XLA Ops:
  0.6 0.8 slice.6
  1.4 0.9 convert_reduce_fusion
  2.3 0.6 and_select_fusion.first_chunk
  2.9 1.4 iota_reduce_fusion
  4.3 1.5 copy.16
  5.8 2.1 copy.18.col_ref
  7.8 3.7 %fusion = (f32[2048,32]{1,0:T(8,128)S(1)}, f32[2048,32]{1,0:T(8,128)S(1)}, f32[2048,32]{1,0:T(8,128)S(1)}) fusion(f32[32]{0:T(128)S(1)} %multiply_exponential_fusion, f32[2048]{0:T(1024)S(1)} %iota_convert_fusion), kind=kLoop, calls=%fused_computation.6 | loop fusion | flops 131072 | bytes 794752 | tf_op jit(solution)/shard_map/neg | solution.py:492
  11.6 1.9 pad_maximum_fusion
  13.5 92.2 %spread.1 = (bf16[2048,1536]{1,0:T(8,128)(2,1)}, bf16[2048,512]{1,0:T(8,128)(2,1)}, bf16[2048,64]{1,0:T(8,128)(2,1)}, bf16[1536,768]{1,0:T(8,128)(2,1)}, bf16[51...) custom-call(bf16[256,768]{1,0:T(8,128)(2,1)} %bitcast.16, bf16[256,256]{1,0:T(8,128)(2,1)} %bitcast.17, ...), custom_call_target="tpu_custom_call" | custom-call | flops 30000001024 | bytes 16000000 | tf_op jit(solution)/shard_map/spread/pallas_call | solution.py:466
  105.7 0.0 copy-start.2
  105.7 37.5 %attend.1 = (bf16[2048,512]{1,0:T(8,128)(2,1)}, f32[4,128]{1,0:T(4,128)}) custom-call(s32[16]{0:T(128)} %bitcast.19, s32[8]{0:T(128)} %and_select_fusion.first_chunk, s32[16]{0:T(128)} %get-tuple-element.14.stored_at, bf16[2048,1536]{1,0:T(8,128)(2,1)} %get-tuple-element.15.query_ref, bf16[2048,512]{1,0:T(8,128)(2,1)} %get-tuple-element.16.key_ref, ...), custom_call_target="tpu_custom_call" | custom-call | flops 12000000000 | bytes 16000000 | tf_op jit(solution)/shard_map/attend/pallas_call | solution.py:500
  143.2 63.7 %give_back.1 = (bf16[256,4096]{1,0:T(8,128)(2,1)}, f32[16,4,128]{2,1,0:T(4,128)}) custom-call(bf16[2048,512]{1,0:T(8,128)(2,1)} %get-tuple-element.21.context_ref, f32[4,128]{1,0:T(4,128)} %get-tuple-element.22.peak_ref), custom_call_target="tpu_custom_call" | custom-call | tf_op jit(solution)/shard_map/give_back/pallas_call | solution.py:524
  206.8 0.8 slice_reduce_fusion
  207.7 0.1 reshape_squeeze.7
  207.8 0.1 broadcast_in_dim.8
  207.9 0.1 broadcast_bitcast_fusion
  207.9 0.1 broadcast_in_dim.7
  208.0 0.1 mul.74
  208.1 0.0 copy-done.2
  208.1 0.9 multiply_convert_fusion.1
  209.0 0.0 copy-done
  209.0 1.9 multiply_convert_fusion
  210.9 0.1 copy-done.1
  211.0 1.3 copy.20
  (7 shorter events, 0.1 us)
Async XLA Ops:
  105.7 102.4 %copy-start.2 = (bf16[64,4096]{1,0:T(8,128)(2,1)S(1)}, bf16[64,4096]{1,0:T(8,128)(2,1)}, u32[]{:S(2)}) copy-start(bf16[64,4096]{1,0:T(8,128)(2,1)} %uk_ref.1) | copy-start | bytes 1572868
  143.2 65.9 %copy-start = (bf16[192,6144]{1,0:T(8,128)(2,1)S(1)}, bf16[192,6144]{1,0:T(8,128)(2,1)}, u32[]{:S(2)}) copy-start(bf16[192,6144]{1,0:T(8,128)(2,1)} %uq_ref.1) | copy-start | bytes 7077892
  209.0 2.0 copy-start.1

commit v3 on v2

--- a/solution.py
+++ b/solution.py
@@ -3,6 +3,7 @@
 
 import jax
 import jax.numpy as jnp
+import numpy as np
 from jax import lax
 from jax.experimental import pallas as pl
 from jax.experimental.pallas import tpu as pltpu
@@ -153,15 +154,17 @@
 
 
 def attend(
-    block, tile, own, order, first_chunk, stored_at,
-    query_ref, key_ref, rope_ref, wq_ref, wk_ref, wv_ref, cos_ref, sin_ref, col_ref, row_ref,
+    block, tile, own, order, labels,
+    query_ref, key_ref, rope_ref, wq_ref, wk_ref, wv_ref, turn_ref, row_ref,
     context_ref, peak_ref,
-    q_s, k_s, v_s, s_s, m_s,
+    q_s, k_s, v_s, s_s, m_s, stored_at,
 ):
     count = query_ref.shape[0]
     scale = 1.0 / math.sqrt(NOPE + ROPE)
     width = NOPE + ROPE
     rows = min(count, 4 * block)
+    for stored in range(count // block):
+        stored_at[order[stored]] = stored
 
     def project(step, unused):
         at = pl.multiple_of(step * rows, rows)
@@ -175,7 +178,7 @@
             lo, hi = part * block, (part + 1) * block
             to = pl.multiple_of(order[step * (rows // block) + part] * block, block)
             there = pl.ds(to, block)
-            cosine, sine = cos_ref[there, :], sin_ref[there, :]
+            cosine, sine = turn_ref[there, :ROPE], turn_ref[there, ROPE:]
             raw = rope_ref[pl.ds(pl.multiple_of(at + lo, block), block), :].astype(jnp.float32)
             key_rope = turned(raw, cosine, sine).astype(jnp.bfloat16)
             v_s[there, :] = value[lo:hi, :]
@@ -192,7 +195,12 @@
     lax.fori_loop(0, count // rows, project, 0)
 
     def per_tile(number, best):
-        first = first_chunk[number]
+        opening = labels[number * tile]
+        first = sum(
+            (labels[(chunk + 1) * tile - 1] < opening).astype(jnp.int32)
+            for chunk in range(count // tile)
+        )
+        own_labels = jnp.transpose(jnp.broadcast_to(row_ref[number], (tile, tile)))
         here = pl.ds(pl.multiple_of(number * tile, tile), tile)
         for head in range(own):
             m_s[head] = jnp.full((tile, 128), masked_value, jnp.float32)
@@ -202,7 +210,7 @@
             gap = (chunk - number) * tile
             later = lax.broadcasted_iota(jnp.int32, (tile, tile), 1) + gap
             now = lax.broadcasted_iota(jnp.int32, (tile, tile), 0)
-            allowed = (later <= now) & (col_ref[here, :] == row_ref[chunk])
+            allowed = (later <= now) & (own_labels == row_ref[chunk])
             for head in range(own):
                 raw = lax.dot_general(
                     q_s[head, here, :], k_s[head, there, :], (((1,), (1,)), ((), ())),
@@ -288,18 +296,21 @@
 ):
     s, t, d = lax.axis_index("seq"), lax.axis_index("tp"), lax.axis_index("dp")
     partner = s + 1 - 2 * lax.rem(s, 2)
-    near = sorted(range(1, n // 2), key=lambda k: (min(k, n // 2 - k), k))
-    same = lambda k: lax.rem(s + 2 * k, n)
-    cross = lambda k: lax.rem(partner + 2 * k, n)
+    parity, level, levels = lax.rem(s, 2), s // 2, n // 2
+    same = lambda z: 2 * z + parity
+    cross = lambda z: 2 * z + 1 - parity
+    turn = lambda k: lax.rem(level + k, levels)
+    within = lambda z: (z >= 0) & (z < levels)
     beside, across, mate = {"tp": 1 - t}, {"dp": 1 - d}, {"seq": partner}
     greet(
         [mate, beside, across]
-        + [{"seq": same(k)} for k in near]
-        + [{"seq": cross(k)} for k in near]
+        + [{"seq": same(turn(k))} for k in range(1, levels)]
+        + [{"seq": cross(turn(k))} for k in range(1, levels)]
     )
     rows, wide = query_ref.shape
     thin = key_ref.shape[1]
     weights = ((uq_ref, wq_out), (uk_ref, wk_out), (uv_ref, wv_out))
+    state = {"when": None}
     started = []
 
     def link(source, target, arrived, where, sender):
@@ -309,9 +320,13 @@
         )
 
     def send(source, target, arrived, where):
-        copy = link(source, target, arrived, where, len(started))
-        copy.start()
-        started.append(copy)
+        link(source, target, arrived, where, len(started)).start()
+        started.append((tuple(source.shape), state["when"]))
+
+    def under(condition, action):
+        state["when"] = condition
+        pl.when(condition)(action)
+        state["when"] = None
 
     def arrive(target, arrived):
         link(target, target, arrived, mate, 0).wait_recv()
@@ -361,10 +376,9 @@
             send(target, target, arrived, across)
 
     own_latents(beside, False)
-    for k in near:
-        own_latents({"seq": same(k)}, True)
-        own_weights(same(k))
-        own_weights(cross(k))
+    for sign in (1, -1):
+        to = level + sign
+        under(within(to), lambda: own_latents({"seq": same(to)}, True))
     own_latents(mate, True)
     own_weights(partner)
     kept = [
@@ -379,24 +393,67 @@
     ]
     for copy in kept:
         copy.start()
-    pass_weights(partner)
-    for k in near:
-        await_latents(same(k), t, True)
-        pass_latents(same(k), t, beside, False)
-        pass_latents(same(k), t, mate, True)
-        pass_weights(same(k))
-        pass_weights(cross(k))
-    for k in [0] + near:
-        await_latents(same(k), 1 - t, False)
-        pass_latents(same(k), 1 - t, mate, False)
-    for k in [0] + near:
-        await_latents(cross(k), t, True)
-        await_latents(cross(k), 1 - t, False)
-    for src in [partner] + [same(k) for k in near] + [cross(k) for k in near]:
-        for index in range(len(weights)):
-            arrive(*weight_spot(index, src, 1 - d))
-    for copy in started:
-        copy.wait_send()
+
+    def from_beside(k):
+        for sign in (1, -1) if k else (1,):
+            source = level - sign * k
+
+            def hand():
+                await_latents(same(source), 1 - t, False)
+                pass_latents(same(source), 1 - t, mate, False)
+
+            under(within(source), hand)
+
+    for k in range(1, levels):
+        for sign in (1, -1):
+            to = level + sign * k
+
+            def far():
+                own_weights(same(to))
+                own_weights(cross(to))
+
+            under(within(to), far)
+        for sign in (1, -1):
+            source, onward = level - sign * k, level + sign
+
+            def take():
+                await_latents(same(source), t, True)
+                pass_latents(same(source), t, beside, False)
+                pass_latents(same(source), t, mate, True)
+
+            under(within(source), take)
+            under(
+                within(source) & within(onward),
+                lambda: pass_latents(same(source), t, {"seq": same(onward)}, True),
+            )
+        if k == 1:
+            pass_weights(partner)
+        for sign in (1, -1):
+            source = level - sign * k
+
+            def relay():
+                pass_weights(same(source))
+                pass_weights(cross(source))
+
+            under(within(source), relay)
+        from_beside(k - 1)
+    from_beside(levels - 1)
+    for k in range(levels):
+        await_latents(cross(turn(k)), t, True)
+        await_latents(cross(turn(k)), 1 - t, False)
+    for k in range(levels):
+        for src in [cross(turn(k))] + ([same(turn(k))] if k else []):
+            for index in range(len(weights)):
+                arrive(*weight_spot(index, src, 1 - d))
+    alike = [target for target, _ in spots(s, t)] + [rope_spot(s)[0]]
+    alike += [weight_spot(index, s, d)[0] for index in range(len(weights))]
+    alike = {tuple(ref.shape): ref for ref in alike}
+    for sender, (shape, condition) in enumerate(started):
+        sent = link(alike[shape], alike[shape], got_rope.at[s], mate, sender)
+        if condition is None:
+            sent.wait_send()
+        else:
+            pl.when(condition)(sent.wait_send)
     for copy in kept:
         copy.wait()
 
@@ -462,7 +519,7 @@
         (devices * w_uv.shape[0], w_uv.shape[1] // devices),
     )
     half = devices // 2
-    copies = 10 * half + 6 * (half - 1) + 3 * half + 6 * (devices - 1)
+    copies = 44 * half
     query, key, rope, wq, wk, wv = pl.pallas_call(
         functools.partial(spread, devices),
         out_shape=[jax.ShapeDtypeStruct(shape, jnp.bfloat16) for shape in shapes],
@@ -487,23 +544,18 @@
     block = count // blocks
     tile = 2 * block
     chunks = count // tile
-    cosine, sine = turning(jnp.arange(count, dtype=jnp.int32), ROPE)
-    cosine = jnp.concatenate([cosine, cosine], axis=1)
-    sine = jnp.concatenate([-sine, sine], axis=1)
-    stored_at = jnp.argmax(
-        order[None, :] == jnp.arange(blocks, dtype=jnp.int32)[:, None], axis=1
-    ).astype(jnp.int32)
-    heads_of = labels[::tile]
-    first_chunk = (
-        jnp.sum((labels[None, :] < heads_of[:, None]).astype(jnp.int32), axis=1) // tile
-    ).astype(jnp.int32)
+    steps = np.arange(ROPE // 2, dtype=np.float32) * np.float32(2.0 / ROPE)
+    freqs = np.exp(np.float32(-math.log(rope_base)) * steps).astype(np.float32)
+    angle = np.arange(count, dtype=np.float32)[:, None] * freqs[None, :]
+    cosine, sine = np.cos(angle), np.sin(angle)
+    turns = jnp.asarray(np.concatenate([cosine, cosine, -sine, sine], axis=1), jnp.float32)
     context, peak = pl.pallas_call(
         functools.partial(attend, block, tile, own),
         out_shape=(
             jax.ShapeDtypeStruct((count, own * VD), jnp.bfloat16),
             jax.ShapeDtypeStruct((own, 128), jnp.float32),
         ),
-        in_specs=[smem] * 3 + [vmem] * 10,
+        in_specs=[smem] * 2 + [vmem] * 8,
         out_specs=(vmem, vmem),
         scratch_shapes=[
             pltpu.VMEM((own, count, NOPE + ROPE), jnp.bfloat16),
@@ -511,6 +563,7 @@
             pltpu.VMEM((count, own * VD), jnp.bfloat16),
             pltpu.VMEM((chunks, own, tile, tile), jnp.float32),
             pltpu.VMEM((own, tile, 128), jnp.float32),
+            pltpu.SMEM((blocks,), jnp.int32),
         ],
         compiler_params=pltpu.CompilerParams(vmem_limit_bytes=60 * 1024 * 1024),
         cost_estimate=pl.CostEstimate(
@@ -518,8 +571,7 @@
         ),
         name="attend",
     )(
-        order, first_chunk, stored_at, query, key, rope, wq, wk, wv, cosine, sine,
-        labels[:, None], labels.reshape(chunks, 1, tile),
+        order, labels, query, key, rope, wq, wk, wv, turns, labels.reshape(chunks, 1, tile),
     )
     context, peaks = pl.pallas_call(
         functools.partial(give_back, devices),

time: 212 us -> 199 us (0.939); the launches traced: 212 us -> 197 us
  other arithmetic: 11.3 us -> 2.79 us
  Pallas kernels: 193 us -> 189 us
  local copies, waits for them, and re-layouts: 7 us -> 4.16 us
    pallas_call x1, Pallas kernels: 92.2 us -> 80.6 us  [by_heads(): pl.pallas_call(functools.partial(spread, devices), out_shape=[jax.ShapeDt...]
    pallas_call x1, Pallas kernels: 63.7 us -> 70.9 us  [by_heads(): pl.pallas_call(functools.partial(give_back, devices), out_shape=[jax.Shap...]
    neg x1 -> x0, other arithmetic: 3.72 us -> none  [by_heads(): sine = jnp.concatenate([-sine, sine], axis=1)]
where the time goes in v3:
time: 199 us; the launch traced here: 197 us
  Pallas kernels  189 us (95%)
  local copies, waits for them, and re-layouts  4.16 us (2%)
  other arithmetic  2.79 us (1%)
    pallas_call x1, Pallas kernels, by_heads(): pl.pallas_call(functools.partial(spread, devices), out_shape=[jax.ShapeDt...  80.6 us
    pallas_call x1, Pallas kernels, by_heads(): pl.pallas_call(functools.partial(give_back, devices), out_shape=[jax.Shap...  70.9 us
    pallas_call x1, Pallas kernels, by_heads(): pl.pallas_call(functools.partial(attend, block, tile, own), out_shape=(ja...  37.6 us

profile of v3, /device:TPU:9, one launch (start us, length us, event | category | flops | bytes accessed | tf_op | source)
XLA Modules:
  0.0 196.7 jit_solution(7506039145441174907)
XLA Ops:
  0.6 1.5 copy.13
  2.1 80.6 %spread.1 = (bf16[2048,1536]{1,0:T(8,128)(2,1)}, bf16[2048,512]{1,0:T(8,128)(2,1)}, bf16[2048,64]{1,0:T(8,128)(2,1)}, bf16[1536,768]{1,0:T(8,128)(2,1)}, bf16[51...) custom-call(bf16[256,768]{1,0:T(8,128)(2,1)} %bitcast.11, bf16[256,256]{1,0:T(8,128)(2,1)} %bitcast.12, ...), custom_call_target="tpu_custom_call" | custom-call | flops 30000001024 | bytes 16000000 | tf_op jit(solution)/shard_map/spread/pallas_call | solution.py:523
  82.7 0.0 copy-start.2
  82.7 37.6 %attend.1 = (bf16[2048,512]{1,0:T(8,128)(2,1)}, f32[4,128]{1,0:T(4,128)}) custom-call(s32[16]{0:T(128)} %bitcast.15, s32[2048]{0:T(1024)} %bitcast.13, bf16[2048,1536]{1,0:T(8,128)(2,1)} %get-tuple-element.13.query_ref, bf16[2048,512]{1,0:T(8,128)(2,1)} %get-tuple-element.14.key_ref, bf16[2048,64]{1,0:T(8,128)(2,1)} %get-tuple-element.15.rope_ref, ...), custom_call_target="tpu_custom_call" | custom-call | flops 12000000000 | bytes 16000000 | tf_op jit(solution)/shard_map/attend/pallas_call | solution.py:552
  120.3 0.0 copy-start
  120.3 70.9 %give_back.1 = (bf16[256,4096]{1,0:T(8,128)(2,1)}, f32[16,4,128]{2,1,0:T(4,128)}) custom-call(bf16[2048,512]{1,0:T(8,128)(2,1)} %get-tuple-element.19.context_ref, f32[4,128]{1,0:T(4,128)} %get-tuple-element.20.peak_ref), custom_call_target="tpu_custom_call" | custom-call | tf_op jit(solution)/shard_map/give_back/pallas_call | solution.py:576
  191.2 0.8 slice_reduce_fusion
  192.0 0.1 reshape_squeeze.7
  192.2 0.1 broadcast_in_dim.8
  192.2 0.1 broadcast_bitcast_fusion
  192.3 0.1 broadcast_in_dim.7
  192.4 0.1 mul.20
  192.5 0.0 copy-done.2
  192.5 0.9 multiply_convert_fusion.1
  193.4 0.0 copy-done
  193.4 0.0 copy-start.1
  193.4 1.9 multiply_convert_fusion
  195.2 0.1 copy-done.1
  195.3 1.3 copy.15
  (3 shorter events, 0.0 us)
Async XLA Ops:
  82.7 109.8 %copy-start.2 = (bf16[64,4096]{1,0:T(8,128)(2,1)S(1)}, bf16[64,4096]{1,0:T(8,128)(2,1)}, u32[]{:S(2)}) copy-start(bf16[64,4096]{1,0:T(8,128)(2,1)} %uk_ref.1) | copy-start | bytes 1572868
  120.3 73.1 %copy-start = (bf16[192,6144]{1,0:T(8,128)(2,1)S(1)}, bf16[192,6144]{1,0:T(8,128)(2,1)}, u32[]{:S(2)}) copy-start(bf16[192,6144]{1,0:T(8,128)(2,1)} %uq_ref.1) | copy-start | bytes 7077892
  193.4 2.0 %copy-start.1 = (bf16[256,4096]{1,0:T(8,128)(2,1)S(1)}, bf16[256,4096]{1,0:T(8,128)(2,1)}, u32[]{:S(2)}) copy-start(bf16[256,4096]{1,0:T(8,128)(2,1)} %get-tuple-element.21) | copy-start | bytes 6291460
